TPU v7x, 32 devices: a whole 2x2x4 slice. The times are simulated.
32 devices in a mesh: row: 8 (over z, x), col: 4 (over y, core).
Axes of the slice: x: 2, y: 2, z: 4, core: 2. Of those that a mesh axis runs over, the one named last changes fastest.
Arguments:
- gradients: bfloat16 [8, 4, 4, 64, 1536], P('row', 'col'), may hold values from -96 to 96
- token_counts: int32 [8, 4], P('row', 'col'), may hold values from 16 to 256
- row_groups: int32 [2, 8, 4], replicated, may hold values from 0 to 3, each once within a row
- col_groups: int32 [1, 4, 8], replicated, may hold values from 0 to 7, each once within a row
Outputs:
- averaged: float32 [8, 4, 4, 64, 1536], P('row', 'col')
- totals: int32 [8, 4], P('row', 'col')
Inputs may be any that keep to these rules, and one draw needn't show every extreme that they name: row_groups[r, i] lists the 4 grid columns in some order: in row round r, grid row i's member of group g sits in column row_groups[r, i, g]. col_groups[0, j] lists the 8 grid rows in some order: grid column j's member of group h sits in row col_groups[0, j, h].
All inputs are finite; a program needn't handle non-finite values.
Results may differ from a plain program's by a relative error of at most 0.0003.
Values may be sent and summed in bfloat16 or wider, within the bound.
A program may use at most 64 MiB of HBM per device.

v0:
```python
import functools

import jax
import jax.numpy as jnp
from jax import lax
from jax.experimental import pallas as pl
from jax.experimental.pallas import tpu as pltpu
from jax.sharding import PartitionSpec as P

MESH = pl.DeviceIdType.MESH
F32 = jnp.float32
SKEW = 2
WIDE = 256
VMEM_GRANT = 48 * 1024 * 1024
LIMIT = 32766.0
FINE = 524200.0
SMALLEST = 1e-33


def path_counts(across, cols, z, table_ref, between_ref, second, third, paths, coef, chosen):
    hops = between_ref.shape[2]

    def into(turn, h, g):
        hits = [(table_ref[turn, g, between_ref[0, j, h]] == j).astype(jnp.int32) for j in range(cols)]
        return functools.reduce(lambda one, two: one + two, hits)

    @pl.loop(0, hops)
    def _(h):
        for g in range(cols):
            second[h, g] = into(0, h, g)
            third[h, g] = into(1, h, g)

    @pl.loop(0, cols)
    def _(k):
        for g in range(cols):
            paths[k, g] = functools.reduce(
                lambda one, two: one + two, [third[h, k] * second[h, g] for h in range(hops)])

    @pl.loop(0, across * cols)
    def _(q):
        i, j = z * across + q // cols, q % cols
        mine = last = jnp.int32(0)
        for g in range(cols):
            mine = jnp.where(table_ref[0, g, i] == j, g, mine)
            last = jnp.where(table_ref[1, g, i] == j, g, last)
        chosen[q] = last
        for k in range(cols):
            coef[q, k] = paths[k, mine]


def encode(value, k, groups, code_ref, step_ref):
    for low in range(0, groups, 4):
        packed = None
        for g in range(low, min(low + 4, groups)):
            part = value(g)
            step = jnp.maximum(jnp.max(jnp.abs(part), axis=0, keepdims=True), SMALLEST) * (1.0 / FINE)
            step_ref[k, g] = step
            code = jnp.round(part * (1.0 / step)).astype(jnp.int32)
            code_ref[k, g] = (code >> 4).astype(jnp.int16)
            bits = (code & 15) << (4 * (g - low))
            packed = bits if packed is None else packed + bits
        code_ref[k, groups + low // 4] = (packed - 32768).astype(jnp.int16)


def decode(k, groups, code_ref, step_ref, value_ref):
    for low in range(0, groups, 4):
        packed = code_ref[k, groups + low // 4].astype(jnp.int32) + 32768
        for g in range(low, min(low + 4, groups)):
            code = code_ref[k, g].astype(jnp.int32) * 16 + ((packed >> (4 * (g - low))) & 15)
            value_ref[k, g] = code.astype(F32) * step_ref[k, g]


def kernel(
    geometry,
    table_ref, between_ref, count_ref, x_ref,
    out_ref, scale_ref, total_ref,
    recv, own, up_sum, down_sum, up_out, up_in, down_out, down_in,
    up_out_step, up_in_step, down_out_step, down_in_step, codes, steps, ret, ret_scale,
    cnt_send, cnt, part_send, parts, inverse, factor,
    second, third, paths, coef, chosen,
    x_send_sem, x_recv_sem, r_send_sem, r_recv_sem, s_send_sem, s_recv_sem, z_send_sem, z_recv_sem, zs_send_sem, zs_recv_sem,
    c_send_sem, c_recv_sem, p_send_sem, p_recv_sem,
):
    across, cols, depth, chunks, wide, groups = geometry
    plane = across * cols
    row, col = lax.axis_index("row"), lax.axis_index("col")
    z = row // across
    me = (row % across) * cols + col

    def member(q):
        return (z * across + q // cols, q % cols)

    def level(other):
        return (other * across + row % across, col)

    def lanes(k):
        return pl.ds(pl.multiple_of(k * wide, 128), wide)

    barrier = pltpu.get_barrier_semaphore()
    for d in range(1, plane):
        pl.semaphore_signal(barrier, inc=1, device_id=member((me + d) % plane), device_id_type=MESH)
    for d in range(1, depth):
        pl.semaphore_signal(barrier, inc=1, device_id=level((z + d) % depth), device_id_type=MESH)
    count = count_ref[0, 0].astype(F32)
    cnt_send[...] = jnp.full(cnt_send.shape, count, F32)
    cnt[me] = jnp.full(cnt_send.shape, count, F32)
    path_counts(across, cols, z, table_ref, between_ref, second, third, paths, coef, chosen)

    @pl.when(z == 0)
    def _():
        up_sum[...] = jnp.zeros(up_sum.shape, F32)

    @pl.when(z == depth - 1)
    def _():
        down_sum[...] = jnp.zeros(down_sum.shape, F32)

    pl.semaphore_wait(barrier, plane + depth - 2)

    def count_copy(d):
        to = (me + d) % plane
        return pltpu.make_async_remote_copy(
            src_ref=cnt_send, dst_ref=cnt.at[me], send_sem=c_send_sem.at[to], recv_sem=c_recv_sem.at[me],
            device_id=member(to), device_id_type=MESH)

    def count_arrival(q):
        return pltpu.make_async_remote_copy(
            src_ref=cnt_send, dst_ref=cnt.at[q], send_sem=c_send_sem.at[q], recv_sem=c_recv_sem.at[q],
            device_id=member(q), device_id_type=MESH)

    def part_copy(d):
        to = (z + d) % depth
        return pltpu.make_async_remote_copy(
            src_ref=part_send, dst_ref=parts.at[z], send_sem=p_send_sem.at[to], recv_sem=p_recv_sem.at[z],
            device_id=level(to), device_id_type=MESH)

    def part_arrival(s):
        return pltpu.make_async_remote_copy(
            src_ref=part_send, dst_ref=parts.at[s], send_sem=p_send_sem.at[s], recv_sem=p_recv_sem.at[s],
            device_id=level(s), device_id_type=MESH)

    def piece_copy(k, to, slot):
        return pltpu.make_async_remote_copy(
            src_ref=x_ref.at[to, :, lanes(k)], dst_ref=recv.at[k, slot],
            send_sem=x_send_sem.at[k, to], recv_sem=x_recv_sem.at[k, slot],
            device_id=member(to), device_id_type=MESH)

    def result_copy(k, to, slot):
        return pltpu.make_async_remote_copy(
            src_ref=ret.at[k, to], dst_ref=out_ref.at[slot, :, lanes(k)],
            send_sem=r_send_sem.at[k, to], recv_sem=r_recv_sem.at[k, slot],
            device_id=member(to), device_id_type=MESH)

    def scale_copy(k, to, slot):
        return pltpu.make_async_remote_copy(
            src_ref=ret_scale.at[k, to], dst_ref=scale_ref.at[slot, :, lanes(k)],
            send_sem=s_send_sem.at[k, to], recv_sem=s_recv_sem.at[k, slot],
            device_id=member(to), device_id_type=MESH)

    def result_local(k):
        return pltpu.make_async_copy(ret.at[k, me], out_ref.at[me, :, lanes(k)], r_recv_sem.at[k, me])

    def scale_local(k):
        return pltpu.make_async_copy(ret_scale.at[k, me], scale_ref.at[me, :, lanes(k)], s_recv_sem.at[k, me])

    def up_step_copy(k):
        return pltpu.make_async_remote_copy(
            src_ref=up_out_step.at[k], dst_ref=up_in_step.at[k],
            send_sem=zs_send_sem.at[0, k], recv_sem=zs_recv_sem.at[0, k],
            device_id=level((z + 1) % depth), device_id_type=MESH)

    def up_copy(k):
        return pltpu.make_async_remote_copy(
            src_ref=up_out.at[k], dst_ref=up_in.at[k], send_sem=z_send_sem.at[0, k], recv_sem=z_recv_sem.at[0, k],
            device_id=level((z + 1) % depth), device_id_type=MESH)

    def down_step_copy(k):
        return pltpu.make_async_remote_copy(
            src_ref=down_out_step.at[k], dst_ref=down_in_step.at[k],
            send_sem=zs_send_sem.at[1, k], recv_sem=zs_recv_sem.at[1, k],
            device_id=level((z + depth - 1) % depth), device_id_type=MESH)

    def down_copy(k):
        return pltpu.make_async_remote_copy(
            src_ref=down_out.at[k], dst_ref=down_in.at[k], send_sem=z_send_sem.at[1, k], recv_sem=z_recv_sem.at[1, k],
            device_id=level((z + depth - 1) % depth), device_id_type=MESH)

    @pl.loop(1, plane)
    def _(d):
        count_copy(d).start()

    @pl.loop(0, chunks)
    def _(k):
        @pl.loop(1, plane)
        def _(d):
            piece_copy(k, (me + d) % plane, me).start()

    @pl.loop(1, plane)
    def _(d):
        count_arrival((me + d) % plane).wait_recv()

    for g in range(groups):
        part = None
        for q in range(plane):
            term = coef[q, g].astype(F32) * cnt[q]
            factor[q, g] = term
            part = term if q == 0 else part + term
        part_send[g] = part
        parts[z, g] = part

    @pl.loop(1, depth)
    def _(d):
        part_copy(d).start()

    far = jnp.maximum(z, depth - 1 - z)

    @pl.loop(0, chunks + SKEW * (depth - 1))
    def _(t):
        @pl.when(t < chunks)
        def _():
            recv[t, me] = x_ref[me, :, lanes(t)]

            @pl.loop(1, plane)
            def _(d):
                piece_copy(t, me, (me + d) % plane).wait_recv()

            sums = [None] * groups
            for q in range(plane):
                piece = recv[t, q].astype(F32)
                for g in range(groups):
                    term = piece * factor[q, g]
                    sums[g] = term if q == 0 else sums[g] + term
            for g in range(groups):
                own[t, g] = sums[g]

        up = t - SKEW * z

        @pl.when((up >= 0) & (up < chunks))
        def _():
            @pl.when(z > 0)
            def _():
                up_copy(up).wait_recv()
                up_step_copy(up).wait_recv()
                decode(up, groups, up_in, up_in_step, up_sum)

            @pl.when(z < depth - 1)
            def _():
                encode(lambda g: own[up, g] + up_sum[up, g], up, groups, up_out, up_out_step)
                up_step_copy(up).start()
                up_copy(up).start()

        down = t - SKEW * (depth - 1 - z)

        @pl.when((down >= 0) & (down < chunks))
        def _():
            @pl.when(z < depth - 1)
            def _():
                down_copy(down).wait_recv()
                down_step_copy(down).wait_recv()
                decode(down, groups, down_in, down_in_step, down_sum)

            @pl.when(z > 0)
            def _():
                encode(lambda g: own[down, g] + down_sum[down, g], down, groups, down_out, down_out_step)
                down_step_copy(down).start()
                down_copy(down).start()

        end = t - SKEW * far

        @pl.when(end == 0)
        def _():
            @pl.loop(1, depth)
            def _(d):
                part_arrival((z + d) % depth).wait_recv()

            for g in range(groups):
                weight = parts[0, g]
                for s in range(1, depth):
                    weight = weight + parts[s, g]
                parts[z, g] = weight
                inverse[g] = 1.0 / weight
            total_ref[...] = parts[z, chosen[me], :, :1].astype(jnp.int32)

        @pl.when((end >= 0) & (end < chunks))
        def _():
            for g in range(groups):
                mean = (own[end, g] + up_sum[end, g] + down_sum[end, g]) * inverse[g]
                step = jnp.maximum(jnp.max(jnp.abs(mean), axis=0, keepdims=True), SMALLEST) * (1.0 / LIMIT)
                steps[g] = step
                codes[g] = jnp.round(mean * (1.0 / step)).astype(jnp.int32).astype(jnp.int16)

            @pl.loop(1, plane, unroll=True)
            def _(d):
                to = (me + d) % plane
                ret[end, to] = codes[chosen[to]]
                ret_scale[end, to] = steps[chosen[to]]
                result_copy(end, to, me).start()
                scale_copy(end, to, me).start()

            ret[end, me] = codes[chosen[me]]
            ret_scale[end, me] = steps[chosen[me]]
            result_local(end).start()
            scale_local(end).start()

    @pl.loop(1, plane)
    def _(d):
        count_copy(d).wait_send()

    @pl.loop(1, depth)
    def _(d):
        part_copy(d).wait_send()

    @pl.loop(0, chunks)
    def _(k):
        @pl.when(z < depth - 1)
        def _():
            up_copy(k).wait_send()
            up_step_copy(k).wait_send()

        @pl.when(z > 0)
        def _():
            down_copy(k).wait_send()
            down_step_copy(k).wait_send()

        @pl.loop(1, plane)
        def _(d):
            piece_copy(k, (me + d) % plane, me).wait_send()
            result_copy(k, (me + d) % plane, me).wait_send()
            result_copy(k, me, (me + d) % plane).wait_recv()
            scale_copy(k, (me + d) % plane, me).wait_send()
            scale_copy(k, me, (me + d) % plane).wait_recv()

        result_local(k).wait()
        scale_local(k).wait()


def local(gradients, token_counts, row_groups, col_groups):
    rows, cols = lax.axis_size("row"), lax.axis_size("col")
    across = 2 if rows % 2 == 0 else 1
    depth, plane = rows // across, across * cols
    width = gradients.shape[-1]
    height = gradients.size // width // plane
    wide = WIDE if width % WIDE == 0 else width
    chunks = width // wide
    groups = cols
    pieces = gradients.reshape(plane, height, width)
    smem = pl.BlockSpec(memory_space=pltpu.SMEM)
    vmem = pl.BlockSpec(memory_space=pltpu.VMEM)
    slab = pltpu.VMEM((chunks, groups, height, wide), F32)
    coded = pltpu.VMEM((chunks, groups + pl.cdiv(groups, 4), height, wide), jnp.int16)
    step = pltpu.VMEM((chunks, groups, 1, wide), F32)
    sem = pltpu.SemaphoreType.DMA
    codes, scales, total = pl.pallas_call(
        functools.partial(kernel, (across, cols, depth, chunks, wide, groups)),
        out_shape=(
            jax.ShapeDtypeStruct((plane, height, width), jnp.int16),
            jax.ShapeDtypeStruct((plane, 1, width), F32),
            jax.ShapeDtypeStruct((1, 1), jnp.int32),
        ),
        in_specs=[smem, smem, smem, vmem],
        out_specs=(vmem, vmem, vmem),
        scratch_shapes=[
            pltpu.VMEM((chunks, plane, height, wide), gradients.dtype),
            slab, slab, slab, coded, coded, coded, coded, step, step, step, step,
            pltpu.VMEM((groups, height, wide), jnp.int16),
            pltpu.VMEM((groups, 1, wide), F32),
            pltpu.VMEM((chunks, plane, height, wide), jnp.int16),
            pltpu.VMEM((chunks, plane, 1, wide), F32),
            pltpu.VMEM((1, wide), F32),
            pltpu.VMEM((plane, 1, wide), F32),
            pltpu.VMEM((groups, 1, wide), F32),
            pltpu.VMEM((depth, groups, 1, wide), F32),
            pltpu.VMEM((groups, 1, wide), F32),
            pltpu.VMEM((plane, groups, 1, wide), F32),
            pltpu.SMEM((rows, groups), jnp.int32),
            pltpu.SMEM((rows, groups), jnp.int32),
            pltpu.SMEM((groups, groups), jnp.int32),
            pltpu.SMEM((plane, groups), jnp.int32),
            pltpu.SMEM((plane,), jnp.int32),
            sem((chunks, plane)), sem((chunks, plane)), sem((chunks, plane)), sem((chunks, plane)),
            sem((chunks, plane)), sem((chunks, plane)),
            sem((2, chunks)), sem((2, chunks)), sem((2, chunks)), sem((2, chunks)),
            sem((plane,)), sem((plane,)), sem((depth,)), sem((depth,)),
        ],
        compiler_params=pltpu.CompilerParams(
            collective_id=0, has_side_effects=True, vmem_limit_bytes=VMEM_GRANT
        ),
    )(jnp.swapaxes(row_groups, 1, 2), col_groups, token_counts, pieces)
    averaged = codes.astype(F32) * scales
    return averaged.reshape(gradients.shape), total


def solution(mesh):
    placed = (P("row", "col", None, None, None), P("row", "col"), P(), P())
    return jax.shard_map(
        local,
        mesh=mesh,
        in_specs=placed,
        out_specs=(P("row", "col", None, None, None), P("row", "col")),
        check_vma=False,
    )
```

profile of v0, /device:TPU:0, one launch (start us, length us, event | category | flops | bytes accessed | tf_op | source)
XLA Modules:
  0.0 46.2 jit_solution(828260648610740588)
XLA Ops:
  1.3 0.0 copy-start
  1.3 1.1 %copy-done = bf16[1,1,4,64,1536]{4,3,2,1,0:T(8,128)(2,1)S(1)} copy-done((bf16[1,1,4,64,1536]{4,3,2,1,0:T(8,128)(2,1)S(1)}, bf16[1,1,4,64,1536]{4,3,2,1,0:T(8,128)(2,1)}, u32[]{:S(2)}) %copy-start) | copy-done | bytes 786456
  2.4 0.0 copy-start.1
  2.4 0.7 %copy-done.1 = s32[2,8,4]{1,2,0:T(4,128)S(1)} copy-done((s32[2,8,4]{1,2,0:T(4,128)S(1)}, s32[2,8,4]{1,2,0:T(4,128)}, u32[]{:S(2)}) %copy-start.1) | copy-done | bytes 280
  3.1 0.0 copy-start.2
  3.1 0.7 %copy-done.2 = s32[1,4,8]{2,1,0:T(4,128)S(1)} copy-done((s32[1,4,8]{2,1,0:T(4,128)S(1)}, s32[1,4,8]{2,1,0:T(4,128)}, u32[]{:S(2)}) %copy-start.2) | copy-done | bytes 152
  3.8 39.3 %shard_map.59 = (s16[8,32,1536]{2,1,0:T(8,128)(2,1)S(1)}, f32[8,1,1536]{2,1,0:T(1,128)S(1)}, s32[1,1]{1,0:T(1,128)}) custom-call(s32[2,4,8]{2,1,0:T(4,128)S(1)} %bitcast.7, s32[1,4,8]{2,1,0:T(4,128)S(1)} %copy-done.2, s32[1,1]{1,0:T(1,128)S(6)} %copy.10.count_ref, bf16[8,32,1536]{2,1,0:T(8,128)(2,1)S(1)} %bitcast.6), custom_call_target="tpu_custom_call" | custom-call | tf_op jit(solution)/shard_map/pallas_call | solution.py:352
  43.1 1.4 %convert_multiply_fusion = f32[8,32,1536]{2,1,0:T(8,128)} fusion(s16[8,32,1536]{2,1,0:T(8,128)(2,1)S(1)} %get-tuple-element.5, f32[8,1536]{1,0:T(8,128)S(1)} %bitcast.9), kind=kLoop, calls=%fused_computation | loop fusion | flops 786432 | bytes 2408448 | tf_op jit(solution)/shard_map/mul | solution.py:388
  (1 shorter events, 0.0 us)
Async XLA Ops:
  1.3 1.1 %copy-start = (bf16[1,1,4,64,1536]{4,3,2,1,0:T(8,128)(2,1)S(1)}, bf16[1,1,4,64,1536]{4,3,2,1,0:T(8,128)(2,1)}, u32[]{:S(2)}) copy-start(bf16[1,1,4,64,1536]{4,3,2,1,0:T(8,128)(2,1)} %param.4) | copy-start | bytes 2359300
  2.4 0.7 %copy-start.1 = (s32[2,8,4]{1,2,0:T(4,128)S(1)}, s32[2,8,4]{1,2,0:T(4,128)}, u32[]{:S(2)}) copy-start(s32[2,8,4]{1,2,0:T(4,128)} %param.6) | copy-start | bytes 772
  3.1 0.7 %copy-start.2 = (s32[1,4,8]{2,1,0:T(4,128)S(1)}, s32[1,4,8]{2,1,0:T(4,128)}, u32[]{:S(2)}) copy-start(s32[1,4,8]{2,1,0:T(4,128)} %between_ref.1) | copy-start | bytes 388
where the time goes:
time: 46.5 us; the launch traced here: 46.2 us
  Pallas kernels  39.3 us (85%)
  between operations  3.04 us (7%)
  local copies, waits for them, and re-layouts  2.5 us (5%)
  other arithmetic  1.42 us (3%)
    pallas_call x1, Pallas kernels, local(): pl.pallas_call(functools.partial(kernel, (across, cols, depth, chunks, wi...  39.3 us
    unnamed x7, local copies, waits for them, and re-layouts  2.5 us
    mul x1, other arithmetic, local(): averaged = codes.astype(F32) * scales  1.42 us

commit v1 on v0

v1 whole, which is shorter than its diff:
```python
import functools

import jax
import jax.numpy as jnp
from jax import lax
from jax.experimental import pallas as pl
from jax.experimental.pallas import tpu as pltpu
from jax.sharding import PartitionSpec as P

MESH = pl.DeviceIdType.MESH
F32 = jnp.float32
WIDE = 256
LEAD = 6.5
CROSS_LAG = 2.2
RETURN_LAG = 4.3
VMEM_GRANT = 48 * 1024 * 1024
LIMIT = 32766.0
FINE = 524200.0
SMALLEST = 1e-33


def add(one, two):
    return one + two


def path_counts(cols, table, between, second, third, paths):
    hops = between.shape[2]

    @pl.loop(0, hops)
    def _(h):
        for g in range(cols):
            for turn, into in ((0, second), (1, third)):
                into[h, g] = functools.reduce(add, [
                    (table[turn, g, between[0, j, h]] == j).astype(jnp.int32) for j in range(cols)])

    @pl.loop(0, cols)
    def _(k):
        for g in range(cols):
            paths[k, g] = functools.reduce(add, [third[h, k] * second[h, g] for h in range(hops)])


def group_of(table, turn, row, col, cols):
    found = jnp.int32(0)
    for g in range(cols):
        found = jnp.where(table[turn, g, row] == col, g, found)
    return found


def encode(sums, k, code_ref, step_ref):
    groups = len(sums)
    for low in range(0, groups, 4):
        packed = None
        for g in range(low, min(low + 4, groups)):
            part = sums[g]
            step = jnp.maximum(jnp.max(jnp.abs(part), axis=0, keepdims=True), SMALLEST) * (1.0 / FINE)
            step_ref[k, g] = step
            code = jnp.round(part * (1.0 / step)).astype(jnp.int32)
            code_ref[k, g] = (code >> 4).astype(jnp.int16)
            bits = (code & 15) << (4 * (g - low))
            packed = bits if packed is None else packed + bits
        code_ref[k, groups + low // 4] = (packed - 32768).astype(jnp.int16)


def decode(groups, code_ref, step_ref):
    values = []
    for low in range(0, groups, 4):
        packed = code_ref[groups + low // 4].astype(jnp.int32) + 32768
        for g in range(low, min(low + 4, groups)):
            code = code_ref[g].astype(jnp.int32) * 16 + ((packed >> (4 * (g - low))) & 15)
            values.append(code.astype(F32) * step_ref[g])
    return values


def kernel(
    geometry,
    table_hbm, between_hbm, count_ref, x_hbm,
    out_ref, scale_ref, total_ref,
    table, between, x_ref,
    recv, own, cross_out, cross_out_step, cross_in, cross_in_step,
    codes, steps, twin_in, twin_in_step, pick, pick_step, ret, ret_scale,
    cnt_out, cnt_in, part_out, part_in, weights, inverse, factor,
    second, third, paths,
    load_sem, x_send_sem, x_recv_sem, n_send_sem, n_recv_sem, p_send_sem, p_recv_sem,
    c_send_sem, c_recv_sem, cs_recv_sem, t_send_sem, t_recv_sem, ts_recv_sem,
    cs_send_sem, ts_send_sem, r_send_sem, r_recv_sem, s_send_sem, s_recv_sem,
):
    across, cols, depth, levels, chunks, wide = geometry
    plane, teams, groups = across * cols, depth // levels, cols
    crew = plane * levels
    row, col = lax.axis_index("row"), lax.axis_index("col")
    z = row // across
    team, deck = z // levels, z % levels
    spot = (row % across) * cols + col
    me = spot * levels + deck

    def at(level, q):
        return (level * across + q // cols, q % cols)

    def member(p):
        return at(team * levels + p % levels, p // levels)

    def fellow(q):
        return at(z, q)

    def ally(d):
        return at((team + d) % teams * levels + deck, spot)

    def twin(d):
        return at(team * levels + (deck + d) % levels, spot)

    def lanes(k):
        return pl.ds(k * wide, wide)

    def remote(src, dst, send_sem, recv_sem, device):
        return pltpu.make_async_remote_copy(
            src_ref=src, dst_ref=dst, send_sem=send_sem, recv_sem=recv_sem, device_id=device, device_id_type=MESH)

    loads = [
        pltpu.make_async_copy(src, dst, load_sem.at[n])
        for n, (src, dst) in enumerate(
            [(x_hbm, x_ref), (table_hbm, table), (between_hbm, between)])]
    for load in loads:
        load.start()

    barrier = pltpu.get_barrier_semaphore()
    for d in range(1, crew):
        pl.semaphore_signal(barrier, inc=1, device_id=member((me + d) % crew), device_id_type=MESH)
    for d in range(1, teams):
        pl.semaphore_signal(barrier, inc=1, device_id=ally(d), device_id_type=MESH)
    count = count_ref[0, 0].astype(F32)
    cnt_out[...] = jnp.full(cnt_out.shape, count, F32)
    loads[0].wait()
    pl.semaphore_wait(barrier, crew + teams - 2)

    def count_copy(d):
        return remote(cnt_out, cnt_in.at[d - 1], n_send_sem, n_recv_sem, member((me + d) % crew))

    def piece_copy(k, d):
        to = (me + d) % crew
        return remote(x_ref.at[to, :, lanes(k)], recv.at[k, d - 1], x_send_sem, x_recv_sem.at[k], member(to))

    def part_copy(d):
        return remote(part_out, part_in.at[d - 1], p_send_sem, p_recv_sem, ally(d))

    def cross_copies(k, d):
        return (
            remote(cross_out_step.at[k], cross_in_step.at[k, d - 1], cs_send_sem, cs_recv_sem.at[k], ally(d)),
            remote(cross_out.at[k], cross_in.at[k, d - 1], c_send_sem, c_recv_sem.at[k], ally(d)))

    def twin_copies(k, d):
        return (
            remote(steps.at[k], twin_in_step.at[k, d - 1], ts_send_sem, ts_recv_sem.at[k], twin(d)),
            remote(codes.at[k], twin_in.at[k, d - 1], t_send_sem, t_recv_sem.at[k], twin(d)))

    def return_copies(k, d):
        to = (spot + d) % plane
        return (
            remote(ret_scale.at[k, d - 1], scale_ref.at[spot, :, :, lanes(k)], s_send_sem, s_recv_sem, fellow(to)),
            remote(ret.at[k, d - 1], out_ref.at[spot, :, :, lanes(k)], r_send_sem, r_recv_sem, fellow(to)))

    def begin(k):
        for d in range(1, crew):
            piece_copy(k, d).start()

    def gather(k):
        remote(recv.at[k], recv.at[k], x_send_sem, x_recv_sem.at[k], member((me + 1) % crew)).wait_recv()
        sums = [None] * groups
        for d in range(crew):
            piece = (x_ref[me, :, lanes(k)] if d == 0 else recv[k, d - 1]).astype(F32)
            for g in range(groups):
                term = piece * factor[d, g]
                sums[g] = term if d == 0 else sums[g] + term
        for g in range(groups):
            own[k, g] = sums[g]
        if teams > 1:
            encode(sums, k, cross_out, cross_out_step)
            for d in range(1, teams):
                for copy in cross_copies(k, d):
                    copy.start()

    def settle():
        if teams > 1:
            remote(part_in, part_in, p_send_sem, p_recv_sem, ally(1)).wait_recv()
        for g in range(groups):
            weight = part_out[g]
            for d in range(1, teams):
                weight = weight + part_in[d - 1, g]
            weights[g] = weight
            inverse[g] = 1.0 / weight
        mine = group_of(table, 1, row, col, cols)
        total_ref[...] = weights[mine, :, :1].astype(jnp.int32)

    def cross(k):
        sums = [own[k, g] for g in range(groups)]
        if teams > 1:
            remote(cross_in_step.at[k], cross_in_step.at[k], cs_send_sem, cs_recv_sem.at[k], ally(1)).wait_recv()
            remote(cross_in.at[k], cross_in.at[k], c_send_sem, c_recv_sem.at[k], ally(1)).wait_recv()
        for d in range(1, teams):
            sums = [a + b for a, b in zip(sums, decode(groups, cross_in.at[k, d - 1], cross_in_step.at[k, d - 1]))]
        for g in range(groups):
            mean = sums[g] * inverse[g]
            step = jnp.maximum(jnp.max(jnp.abs(mean), axis=0, keepdims=True), SMALLEST) * (1.0 / LIMIT)
            steps[k, g] = step
            codes[k, g] = jnp.round(mean * (1.0 / step)).astype(jnp.int32).astype(jnp.int16)
        for d in range(1, levels):
            for copy in twin_copies(k, d):
                copy.start()

    def give(k):
        if levels > 1:
            remote(twin_in_step.at[k], twin_in_step.at[k], ts_send_sem, ts_recv_sem.at[k], twin(1)).wait_recv()
            remote(twin_in.at[k], twin_in.at[k], t_send_sem, t_recv_sem.at[k], twin(1)).wait_recv()
            for d in range(1, levels):
                for g in range(groups):
                    pick[d - 1, g] = twin_in[k, d - 1, g]
                    pick_step[d - 1, g] = twin_in_step[k, d - 1, g]
        for d in range(plane):
            g = group_of(table, 1, *fellow((spot + d) % plane), cols)
            for l in range(levels):
                code = codes[k, g] if l == 0 else pick[l - 1, g]
                step = steps[k, g] if l == 0 else pick_step[l - 1, g]
                home = (deck + levels - l) % levels
                if d == 0:
                    out_ref[spot, home, :, lanes(k)] = code
                    scale_ref[spot, home, :, lanes(k)] = step
                else:
                    ret[k, d - 1, home] = code
                    ret_scale[k, d - 1, home] = step
            if d > 0:
                for copy in return_copies(k, d):
                    copy.start()

    for d in range(1, crew):
        count_copy(d).start()
    plan = []
    for k in range(chunks):
        plan.append((k - LEAD, 0, begin, k))
        plan.append((k, 3, gather, k))
        plan.append((k + CROSS_LAG, 2, cross, k))
        plan.append((k + RETURN_LAG, 1, give, k))
    plan.sort(key=lambda entry: (entry[0], entry[1]))
    early = [entry for entry in plan if entry[0] < 0]
    for _, _, action, k in early:
        action(k)

    loads[1].wait()
    loads[2].wait()
    path_counts(cols, table, between, second, third, paths)
    remote(cnt_in, cnt_in, n_send_sem, n_recv_sem, member((me + 1) % crew)).wait_recv()
    parts = [None] * groups
    for d in range(crew):
        i, j = member((me + crew - d) % crew)
        first = group_of(table, 0, i, j, cols)
        tally = cnt_out[...] if d == 0 else cnt_in[d - 1]
        for g in range(groups):
            term = paths[g, first].astype(F32) * tally
            factor[d, g] = term
            parts[g] = term if d == 0 else parts[g] + term
    for g in range(groups):
        part_out[g] = parts[g]
    for d in range(1, teams):
        part_copy(d).start()

    settled = False
    for _, _, action, k in plan[len(early):]:
        if action is cross and not settled:
            settle()
            settled = True
        action(k)

    member_any, team_any, twin_any, fellow_any = member((me + 1) % crew), ally(1), twin(1), fellow((spot + 1) % plane)
    remote(cnt_in, cnt_in, n_send_sem, n_recv_sem, member_any).wait_send()
    remote(recv, recv, x_send_sem, x_recv_sem.at[0], member_any).wait_send()
    if teams > 1:
        remote(part_in, part_in, p_send_sem, p_recv_sem, team_any).wait_send()
        remote(cross_in_step, cross_in_step, cs_send_sem, cs_recv_sem.at[0], team_any).wait_send()
        remote(cross_in, cross_in, c_send_sem, c_recv_sem.at[0], team_any).wait_send()
    if levels > 1:
        remote(twin_in_step, twin_in_step, ts_send_sem, ts_recv_sem.at[0], twin_any).wait_send()
        remote(twin_in, twin_in, t_send_sem, t_recv_sem.at[0], twin_any).wait_send()
    scales = remote(ret_scale, scale_ref.at[pl.ds(0, plane - 1)], s_send_sem, s_recv_sem, fellow_any)
    results = remote(ret, out_ref.at[pl.ds(0, plane - 1)], r_send_sem, r_recv_sem, fellow_any)
    for arrival in (scales, results):
        arrival.wait_send()
        arrival.wait_recv()


def local(gradients, token_counts, row_groups, col_groups):
    rows, cols = lax.axis_size("row"), lax.axis_size("col")
    across = 2 if rows % 2 == 0 else 1
    depth, plane = rows // across, across * cols
    width = gradients.shape[-1]
    lines = gradients.size // width
    levels = 2 if depth % 2 == 0 and lines % (2 * plane * 16) == 0 else 1
    teams, crew = depth // levels, levels * plane
    height = lines // crew
    wide = WIDE if width % WIDE == 0 else width
    chunks = width // wide
    groups = cols
    pieces = gradients.reshape(crew, height, width)
    hbm = pl.BlockSpec(memory_space=pltpu.HBM)
    smem = pl.BlockSpec(memory_space=pltpu.SMEM)
    stay = functools.partial(pltpu.with_memory_space_constraint, memory_space=pltpu.HBM)
    vmem = pl.BlockSpec(memory_space=pltpu.VMEM)
    others, mates = max(teams - 1, 1), max(levels - 1, 1)
    coded = groups + pl.cdiv(groups, 4)
    sem = pltpu.SemaphoreType.DMA
    codes, scales, total = pl.pallas_call(
        functools.partial(kernel, (across, cols, depth, levels, chunks, wide)),
        out_shape=(
            jax.ShapeDtypeStruct((plane, levels, height, width), jnp.int16),
            jax.ShapeDtypeStruct((plane, levels, 1, width), F32),
            jax.ShapeDtypeStruct((1, 1), jnp.int32),
        ),
        in_specs=[hbm, hbm, smem, hbm],
        out_specs=(vmem, vmem, vmem),
        scratch_shapes=[
            pltpu.SMEM((2, cols, rows), jnp.int32),
            pltpu.SMEM((1, cols, rows), jnp.int32),
            pltpu.VMEM((crew, height, width), gradients.dtype),
            pltpu.VMEM((chunks, crew - 1, height, wide), gradients.dtype),
            pltpu.VMEM((chunks, groups, height, wide), F32),
            pltpu.VMEM((chunks, coded, height, wide), jnp.int16),
            pltpu.VMEM((chunks, groups, 1, wide), F32),
            pltpu.VMEM((chunks, others, coded, height, wide), jnp.int16),
            pltpu.VMEM((chunks, others, groups, 1, wide), F32),
            pltpu.VMEM((chunks, groups, height, wide), jnp.int16),
            pltpu.VMEM((chunks, groups, 1, wide), F32),
            pltpu.VMEM((chunks, mates, groups, height, wide), jnp.int16),
            pltpu.VMEM((chunks, mates, groups, 1, wide), F32),
            pltpu.VMEM((mates, groups, height, wide), jnp.int16),
            pltpu.VMEM((mates, groups, 1, wide), F32),
            pltpu.VMEM((chunks, plane - 1, levels, height, wide), jnp.int16),
            pltpu.VMEM((chunks, plane - 1, levels, 1, wide), F32),
            pltpu.VMEM((1, wide), F32),
            pltpu.VMEM((crew - 1, 1, wide), F32),
            pltpu.VMEM((groups, 1, wide), F32),
            pltpu.VMEM((others, groups, 1, wide), F32),
            pltpu.VMEM((groups, 1, wide), F32),
            pltpu.VMEM((groups, 1, wide), F32),
            pltpu.VMEM((crew, groups, 1, wide), F32),
            pltpu.SMEM((rows, groups), jnp.int32),
            pltpu.SMEM((rows, groups), jnp.int32),
            pltpu.SMEM((groups, groups), jnp.int32),
            sem((3,)), sem, sem((chunks,)), sem, sem, sem, sem,
            sem, sem((chunks,)), sem((chunks,)), sem, sem((chunks,)), sem((chunks,)),
            sem, sem, sem, sem, sem, sem,
        ],
        compiler_params=pltpu.CompilerParams(
            collective_id=0, has_side_effects=True, vmem_limit_bytes=VMEM_GRANT
        ),
    )(stay(jnp.swapaxes(row_groups, 1, 2)), stay(col_groups), token_counts, stay(pieces))
    averaged = codes.astype(F32) * scales
    return averaged.reshape(gradients.shape), total


def solution(mesh):
    placed = (P("row", "col", None, None, None), P("row", "col"), P(), P())
    return jax.shard_map(
        local,
        mesh=mesh,
        in_specs=placed,
        out_specs=(P("row", "col", None, None, None), P("row", "col")),
        check_vma=False,
    )
```

time: 46.5 us -> 38.1 us (0.82)
  Pallas kernels: 39.3 us -> 33.4 us
  local copies, waits for them, and re-layouts: 2.5 us -> 0.05 us
    pallas_call x1, Pallas kernels: 39.3 us -> 33.4 us  [local(): pl.pallas_call(functools.partial(kernel, (across, cols, depth, levels, ch...]
    unnamed x7 -> x1, local copies, waits for them, and re-layouts: 2.5 us -> 0.05 us
where the time goes in v1:
time: 38.1 us; the launch traced here: 37.9 us
  Pallas kernels  33.4 us (88%)
  between operations  2.98 us (8%)
  other arithmetic  1.41 us (4%)
    pallas_call x1, Pallas kernels, local(): pl.pallas_call(functools.partial(kernel, (across, cols, depth, levels, ch...  33.4 us
    mul x1, other arithmetic, local(): averaged = codes.astype(F32) * scales  1.41 us

profile of v1, /device:TPU:0, one launch (start us, length us, event | category | flops | bytes accessed | tf_op | source)
XLA Modules:
  0.0 37.9 jit_solution(16237612669254681978)
XLA Ops:
  1.3 33.4 %shard_map.59 = (s16[8,2,16,1536]{3,2,1,0:T(8,128)(2,1)S(1)}, f32[8,2,1,1536]{3,2,1,0:T(1,128)S(1)}, s32[1,1]{1,0:T(1,128)}) custom-call(s32[2,4,8]{2,1,0:T(4,128)} %bitcast.9, s32[1,4,8]{2,1,0:T(4,128)} %between_hbm.1, s32[1,1]{1,0:T(1,128)S(6)} %copy.10.count_ref, bf16[16,16,1536]{2,1,0:T(8,128)(2,1)} %bitcast.7), custom_call_target="tpu_custom_call" | custom-call | tf_op jit(solution)/shard_map/pallas_call | solution.py:308
  34.7 0.1 copy.8
  34.8 1.4 %convert_multiply_fusion = f32[8,2,16,1536]{3,2,1,0:T(8,128)} fusion(s16[8,2,16,1536]{3,2,1,0:T(8,128)(2,1)S(1)} %get-tuple-element.5, f32[8,2,1536]{2,1,0:T(2,128)S(1)} %bitcast.8), kind=kLoop, calls=%fused_computation | loop fusion | flops 786432 | bytes 2457600 | tf_op jit(solution)/shard_map/mul | solution.py:353

commit v2 on v1

v2 whole, which is shorter than its diff:
```python
import functools

import jax
import jax.numpy as jnp
from jax import lax
from jax.experimental import pallas as pl
from jax.experimental.pallas import tpu as pltpu
from jax.sharding import PartitionSpec as P

MESH = pl.DeviceIdType.MESH
F32 = jnp.float32
WIDE = 256
JOINED = ()
TWINNED = (0, 1)
LEAD = 6.5
JOIN_LAG = 2.2
CROSS_LAG = 2.6
TWIN_LAG = 2.2
VMEM_GRANT = 48 * 1024 * 1024
LIMIT = 32766.0
SMALLEST = 1e-33
LANES = 128


def add(one, two):
    return one + two


def path_counts(cols, table, between, second, third, paths):
    hops = between.shape[2]

    @pl.loop(0, hops)
    def _(h):
        for g in range(cols):
            for turn, into in ((0, second), (1, third)):
                into[h, g] = functools.reduce(add, [
                    (table[turn, g, between[0, j, h]] == j).astype(jnp.int32) for j in range(cols)])

    @pl.loop(0, cols)
    def _(k):
        for g in range(cols):
            paths[k, g] = functools.reduce(add, [third[h, k] * second[h, g] for h in range(hops)])


def group_of(table, turn, row, col, cols):
    found = jnp.int32(0)
    for g in range(cols):
        found = jnp.where(table[turn, g, row] == col, g, found)
    return found


def spread(row, wide):
    return jnp.concatenate([row] * (wide // LANES), axis=1)


def quantize(part):
    wide = part.shape[1]
    top = jnp.max(jnp.abs(part), axis=0, keepdims=True)
    top = functools.reduce(jnp.maximum, [top[:, low:low + LANES] for low in range(0, wide, LANES)])
    step = jnp.maximum(top, SMALLEST) * (1.0 / LIMIT)
    return jnp.round(part * spread(1.0 / step, wide)).astype(jnp.int32).astype(jnp.int16), step


def encode(sums, code_ref, step_ref):
    for g, part in enumerate(sums):
        code_ref[g], step_ref[g] = quantize(part)


def decode(groups, code_ref, step_ref):
    wide = code_ref.shape[-1]
    return [code_ref[g].astype(F32) * spread(step_ref[g], wide) for g in range(groups)]


def kernel(
    geometry,
    table_hbm, between_hbm, count_ref, x_hbm,
    out_ref, scale_ref, total_ref,
    table, between, x_ref,
    recv, recv_raw, own, join_out, join_out_step, join_in, join_in_step, cross_out, cross_out_step, cross_in, cross_in_step,
    codes, steps, ret, ret_scale, twin_out, twin_out_step, twin_in, twin_in_step, pick, pick_step, pair, pair_scale,
    cnt_out, cnt_in, deal_out, deal_in, weights, inverse, factor,
    second, third, paths, chosen,
    load_sem, x_send_sem, x_recv_sem, n_send_sem, n_recv_sem, d_send_sem, d_recv_sem,
    j_send_sem, j_recv_sem, js_send_sem, js_recv_sem,
    c_send_sem, c_recv_sem, cs_send_sem, cs_recv_sem, t_send_sem, t_recv_sem, ts_send_sem, ts_recv_sem,
    r_send_sem, r_recv_sem, s_send_sem, s_recv_sem, b_send_sem, b_recv_sem, bs_send_sem, bs_recv_sem,
):
    across, cols, depth, levels, chunks, joined, twinned, wide = geometry
    crew = levels * across * cols
    slot = {k: (joined.index(k) if k in joined else k - sum(j < k for j in joined)) for k in range(chunks)}
    berth = {k: (twinned.index(k) if k in twinned else k - sum(j < k for j in twinned)) for k in range(chunks)}
    plane, teams, groups = across * cols, depth // levels, cols
    row, col = lax.axis_index("row"), lax.axis_index("col")
    z = row // across
    team, deck = z // levels, z % levels
    spot = (row % across) * cols + col

    def at(level, q):
        return (level * across + q // cols, q % cols)

    def fellow(q):
        return at(z, q)

    def mate(n):
        return at(team * levels + (deck + n // plane) % levels, (spot + n) % plane)

    def ally(d):
        return at((team + d) % teams * levels + deck, spot)

    def twin(d):
        return at(team * levels + (deck + d) % levels, spot)

    def lanes(k):
        return pl.ds(k * wide, wide)

    def remote(src, dst, send_sem, recv_sem, device):
        return pltpu.make_async_remote_copy(
            src_ref=src, dst_ref=dst, send_sem=send_sem, recv_sem=recv_sem, device_id=device, device_id_type=MESH)

    loads = [
        pltpu.make_async_copy(src, dst, load_sem.at[n])
        for n, (src, dst) in enumerate(
            [(x_hbm, x_ref), (table_hbm, table), (between_hbm, between)])]
    for load in loads:
        load.start()

    barrier = pltpu.get_barrier_semaphore()
    for n in range(1, crew):
        pl.semaphore_signal(barrier, inc=1, device_id=mate(n), device_id_type=MESH)
    for d in range(1, teams):
        pl.semaphore_signal(barrier, inc=1, device_id=ally(d), device_id_type=MESH)
    cnt_out[...] = count_ref[...]
    loads[0].wait()
    pl.semaphore_wait(barrier, crew + teams - 2)

    def strips(k):
        return pl.ds(k * LANES, LANES)

    def count_copy(n):
        return remote(cnt_out, cnt_in.at[n - 1], n_send_sem, n_recv_sem, mate(n))

    def piece_copy(k, d):
        to = (spot + d) % plane
        return remote(x_ref.at[to, :, :, lanes(k)], recv.at[slot[k], d - 1], x_send_sem, x_recv_sem.at[k], fellow(to))

    def raw_copy(k, n):
        source = x_ref.at[(spot + n) % plane, (deck + n // plane) % levels, :, lanes(k)]
        return remote(source, recv_raw.at[slot[k], n - 1], x_send_sem, x_recv_sem.at[k], mate(n))

    def deal_copy(d):
        return remote(deal_out, deal_in.at[d - 1], d_send_sem, d_recv_sem, ally(d))

    def join_copies(k, d):
        return (
            remote(join_out_step.at[slot[k], d - 1], join_in_step.at[slot[k], d - 1], js_send_sem, js_recv_sem.at[slot[k]], twin(d)),
            remote(join_out.at[slot[k], d - 1], join_in.at[slot[k], d - 1], j_send_sem, j_recv_sem.at[slot[k]], twin(d)))

    def cross_copies(k, d):
        return (
            remote(cross_out_step.at[k], cross_in_step.at[k, d - 1], cs_send_sem, cs_recv_sem.at[k], ally(d)),
            remote(cross_out.at[k], cross_in.at[k, d - 1], c_send_sem, c_recv_sem.at[k], ally(d)))

    def return_copies(k, n):
        i = berth[k]
        return (
            remote(ret_scale.at[i, n - 1], scale_ref.at[spot, deck, :, strips(k)], s_send_sem, s_recv_sem, mate(n)),
            remote(ret.at[i, n - 1], out_ref.at[spot, deck, :, lanes(k)], r_send_sem, r_recv_sem, mate(n)))

    def twin_copies(k, d):
        i = berth[k]
        return (
            remote(twin_out_step.at[i], twin_in_step.at[i, d - 1], ts_send_sem, ts_recv_sem.at[i], twin(d)),
            remote(twin_out.at[i], twin_in.at[i, d - 1], t_send_sem, t_recv_sem.at[i], twin(d)))

    def pair_copies(k, d):
        i, to = berth[k], fellow((spot + d) % plane)
        return (
            remote(pair_scale.at[i, d - 1], scale_ref.at[spot, :, :, strips(k)], bs_send_sem, bs_recv_sem, to),
            remote(pair.at[i, d - 1], out_ref.at[spot, :, :, lanes(k)], b_send_sem, b_recv_sem, to))

    def begin(k):
        if k not in joined:
            for n in range(1, crew):
                raw_copy(k, n).start()
        else:
            for d in range(1, plane):
                piece_copy(k, d).start()

    def gather_raw(k):
        remote(recv_raw.at[slot[k]], recv_raw.at[slot[k]], x_send_sem, x_recv_sem.at[k], fellow_any).wait_recv()
        sums = weigh([x_ref[spot, deck, :, lanes(k)] if n == 0 else recv_raw[slot[k], n - 1] for n in range(crew)])
        for g in range(groups):
            own[k, g] = sums[g]
        send_cross(k, sums)

    def weigh(pieces):
        sums = [None] * groups
        for n, piece in enumerate(pieces):
            piece = piece.astype(F32)
            for g in range(groups):
                term = piece * factor[n, g]
                sums[g] = term if n == 0 else sums[g] + term
        return sums

    def send_cross(k, sums):
        if teams > 1:
            encode(sums, cross_out.at[k], cross_out_step.at[k])
            for d in range(1, teams):
                for copy in cross_copies(k, d):
                    copy.start()

    def gather(k):
        remote(recv.at[slot[k]], recv.at[slot[k]], x_send_sem, x_recv_sem.at[k], fellow_any).wait_recv()
        for o in reversed(range(levels)):
            rows = (deck + o) % levels
            sums = weigh(
                [x_ref[spot, rows, :, lanes(k)] if d == 0 else recv[slot[k], d - 1, rows] for d in range(plane)])
            if o > 0:
                encode(sums, join_out.at[slot[k], o - 1], join_out_step.at[slot[k], o - 1])
                for copy in join_copies(k, o):
                    copy.start()
            else:
                for g in range(groups):
                    own[k, g] = sums[g]

    def join(k):
        sums = [own[k, g] for g in range(groups)]
        if levels > 1:
            remote(join_in_step.at[slot[k]], join_in_step.at[slot[k]], js_send_sem, js_recv_sem.at[slot[k]], twin(1)).wait_recv()
            remote(join_in.at[slot[k]], join_in.at[slot[k]], j_send_sem, j_recv_sem.at[slot[k]], twin(1)).wait_recv()
            for d in range(1, levels):
                sums = [a + b for a, b in zip(sums, decode(groups, join_in.at[slot[k], d - 1], join_in_step.at[slot[k], d - 1]))]
            for g in range(groups):
                own[k, g] = sums[g]
        send_cross(k, sums)

    def settle():
        if teams > 1:
            remote(deal_in, deal_in, d_send_sem, d_recv_sem, ally(1)).wait_recv()
        for g in range(groups):
            weight = deal_out[g]
            for d in range(1, teams):
                weight = weight + deal_in[d - 1, g]
            weights[g] = weight
            inverse[g] = 1.0 / weight
        total_ref[...] = weights[chosen[0]]

    def cross(k):
        sums = [own[k, g] for g in range(groups)]
        if teams > 1:
            remote(cross_in_step.at[k], cross_in_step.at[k], cs_send_sem, cs_recv_sem.at[k], ally(1)).wait_recv()
            remote(cross_in.at[k], cross_in.at[k], c_send_sem, c_recv_sem.at[k], ally(1)).wait_recv()
        for d in range(1, teams):
            sums = [a + b for a, b in zip(sums, decode(groups, cross_in.at[k, d - 1], cross_in_step.at[k, d - 1]))]
        i = berth[k]
        for g in range(groups):
            code, step = quantize(sums[g] * spread(inverse[g], wide))
            if k in twinned:
                twin_out[i, g], twin_out_step[i, g] = code, step
            else:
                codes[g], steps[g] = code, step
        if k in twinned:
            for d in range(1, levels):
                for copy in twin_copies(k, d):
                    copy.start()
            return
        for n in range(1, crew):
            ret[i, n - 1] = codes[chosen[n]]
            ret_scale[i, n - 1] = steps[chosen[n]]
            for copy in return_copies(k, n):
                copy.start()
        out_ref[spot, deck, :, lanes(k)] = codes[chosen[0]]
        scale_ref[spot, deck, :, strips(k)] = steps[chosen[0]]

    def give(k):
        i = berth[k]
        remote(twin_in_step.at[i], twin_in_step.at[i], ts_send_sem, ts_recv_sem.at[i], twin(1)).wait_recv()
        remote(twin_in.at[i], twin_in.at[i], t_send_sem, t_recv_sem.at[i], twin(1)).wait_recv()
        for g in range(groups):
            pick[0, g], pick_step[0, g] = twin_out[i, g], twin_out_step[i, g]
            for d in range(1, levels):
                pick[d, g], pick_step[d, g] = twin_in[i, d - 1, g], twin_in_step[i, d - 1, g]
        for d in range(plane):
            for l in range(levels):
                home = (deck + levels - l) % levels
                code, step = pick[l, chosen[d]], pick_step[l, chosen[d]]
                if d == 0:
                    out_ref[spot, home, :, lanes(k)] = code
                    scale_ref[spot, home, :, strips(k)] = step
                else:
                    pair[i, d - 1, home] = code
                    pair_scale[i, d - 1, home] = step
            if d > 0:
                for copy in pair_copies(k, d):
                    copy.start()

    fellow_any = fellow((spot + 1) % plane)
    for n in range(1, crew):
        count_copy(n).start()
    plan = []
    for k in range(chunks):
        plan.append((k - LEAD, 0, begin, k))
        lag = k
        if k in joined:
            plan.append((lag, 4, gather, k))
            lag += JOIN_LAG
            plan.append((lag, 3, join, k))
        else:
            plan.append((lag, 4, gather_raw, k))
        lag += CROSS_LAG
        plan.append((lag, 2, cross, k))
        if k in twinned:
            plan.append((lag + TWIN_LAG, 1, give, k))
    plan.sort(key=lambda entry: (entry[0], entry[1]))
    early = [entry for entry in plan if entry[0] < 0]
    for _, _, action, k in early:
        action(k)

    loads[1].wait()
    loads[2].wait()
    path_counts(cols, table, between, second, third, paths)
    remote(cnt_in, cnt_in, n_send_sem, n_recv_sem, fellow_any).wait_recv()
    for n in range(crew):
        chosen[n] = group_of(table, 1, *mate(n), cols)
    parts = [None] * groups
    for n in range(crew):
        i, j = at(team * levels + (deck + levels - n // plane) % levels, (spot + plane - n % plane) % plane)
        first = group_of(table, 0, i, j, cols)
        tally = cnt_out[...] if n == 0 else cnt_in[n - 1]
        for g in range(groups):
            term = paths[g, first].astype(F32) * tally
            factor[n, g] = spread(term, wide)
            parts[g] = term if n == 0 else parts[g] + term
    for g in range(groups):
        deal_out[g] = parts[g]
    for d in range(1, teams):
        deal_copy(d).start()

    seen = set()
    for _, _, action, k in plan[len(early):]:
        if action is cross and cross not in seen:
            settle()
        seen.add(action)
        action(k)

    remote(cnt_in, cnt_in, n_send_sem, n_recv_sem, fellow_any).wait_send()
    drains = []
    if len(joined) < chunks:
        drains.append((recv_raw, x_send_sem, x_recv_sem.at[0], fellow_any))
    if joined:
        drains += [
            (recv, x_send_sem, x_recv_sem.at[0], fellow_any), (join_in_step, js_send_sem, js_recv_sem.at[0], twin(1)),
            (join_in, j_send_sem, j_recv_sem.at[0], twin(1))]
    if teams > 1:
        drains += [
            (deal_in, d_send_sem, d_recv_sem, ally(1)), (cross_in_step, cs_send_sem, cs_recv_sem.at[0], ally(1)),
            (cross_in, c_send_sem, c_recv_sem.at[0], ally(1))]
    if twinned:
        drains += [
            (twin_in_step, ts_send_sem, ts_recv_sem.at[0], twin(1)), (twin_in, t_send_sem, t_recv_sem.at[0], twin(1))]
    for ref, send_sem, recv_sem, device in drains:
        remote(ref, ref, send_sem, recv_sem, device).wait_send()
    arrivals = []
    if len(twinned) < chunks:
        arrivals += [(ret_scale, s_send_sem, s_recv_sem), (ret, r_send_sem, r_recv_sem)]
    if twinned:
        arrivals += [(pair_scale, bs_send_sem, bs_recv_sem), (pair, b_send_sem, b_recv_sem)]
    for ref, send_sem, recv_sem in arrivals:
        remote(ref, ref, send_sem, recv_sem, fellow_any).wait_send()
        remote(ref, ref, send_sem, recv_sem, fellow_any).wait_recv()


def local(gradients, token_counts, row_groups, col_groups):
    rows, cols = lax.axis_size("row"), lax.axis_size("col")
    across = 2 if rows % 2 == 0 else 1
    depth, plane = rows // across, across * cols
    width = gradients.shape[-1]
    lines = gradients.size // width
    levels = 2 if depth % 2 == 0 and lines % (2 * plane * 16) == 0 else 1
    teams = depth // levels
    height = lines // (plane * levels)
    wide = WIDE if width % WIDE == 0 else LANES
    chunks = width // wide
    groups = cols
    counts = jnp.broadcast_to(token_counts.astype(F32), (1, LANES))
    pieces = gradients.reshape(plane, levels, height, width)
    hbm = pl.BlockSpec(memory_space=pltpu.HBM)
    stay = functools.partial(pltpu.with_memory_space_constraint, memory_space=pltpu.HBM)
    vmem = pl.BlockSpec(memory_space=pltpu.VMEM)
    others, mates = max(teams - 1, 1), max(levels - 1, 1)
    joined = tuple(k for k in JOINED if k < chunks and levels > 1)
    twinned = tuple(k for k in TWINNED if k < chunks and levels > 1)
    rest, raw = max(len(joined), 1), max(chunks - len(joined), 1)
    paired, single = max(len(twinned), 1), max(chunks - len(twinned), 1)
    crew = levels * plane
    sem = pltpu.SemaphoreType.DMA
    codes, scales, total = pl.pallas_call(
        functools.partial(kernel, (across, cols, depth, levels, chunks, joined, twinned, wide)),
        out_shape=(
            jax.ShapeDtypeStruct((plane, levels, height, width), jnp.int16),
            jax.ShapeDtypeStruct((plane, levels, 1, chunks * LANES), F32),
            jax.ShapeDtypeStruct((1, LANES), F32),
        ),
        in_specs=[hbm, hbm, vmem, hbm],
        out_specs=(vmem, vmem, vmem),
        scratch_shapes=[
            pltpu.SMEM((2, cols, rows), jnp.int32),
            pltpu.SMEM((1, cols, rows), jnp.int32),
            pltpu.VMEM((plane, levels, height, width), gradients.dtype),
            pltpu.VMEM((rest, plane - 1, levels, height, wide), gradients.dtype),
            pltpu.VMEM((raw, crew - 1, height, wide), gradients.dtype),
            pltpu.VMEM((chunks, groups, height, wide), F32),
            pltpu.VMEM((rest, mates, groups, height, wide), jnp.int16),
            pltpu.VMEM((rest, mates, groups, 1, LANES), F32),
            pltpu.VMEM((rest, mates, groups, height, wide), jnp.int16),
            pltpu.VMEM((rest, mates, groups, 1, LANES), F32),
            pltpu.VMEM((chunks, groups, height, wide), jnp.int16),
            pltpu.VMEM((chunks, groups, 1, LANES), F32),
            pltpu.VMEM((chunks, others, groups, height, wide), jnp.int16),
            pltpu.VMEM((chunks, others, groups, 1, LANES), F32),
            pltpu.VMEM((groups, height, wide), jnp.int16),
            pltpu.VMEM((groups, 1, LANES), F32),
            pltpu.VMEM((single, crew - 1, height, wide), jnp.int16),
            pltpu.VMEM((single, crew - 1, 1, LANES), F32),
            pltpu.VMEM((paired, groups, height, wide), jnp.int16),
            pltpu.VMEM((paired, groups, 1, LANES), F32),
            pltpu.VMEM((paired, mates, groups, height, wide), jnp.int16),
            pltpu.VMEM((paired, mates, groups, 1, LANES), F32),
            pltpu.VMEM((levels, groups, height, wide), jnp.int16),
            pltpu.VMEM((levels, groups, 1, LANES), F32),
            pltpu.VMEM((paired, plane - 1, levels, height, wide), jnp.int16),
            pltpu.VMEM((paired, plane - 1, levels, 1, LANES), F32),
            pltpu.VMEM((1, LANES), F32),
            pltpu.VMEM((crew - 1, 1, LANES), F32),
            pltpu.VMEM((groups, 1, LANES), F32),
            pltpu.VMEM((others, groups, 1, LANES), F32),
            pltpu.VMEM((groups, 1, LANES), F32),
            pltpu.VMEM((groups, 1, LANES), F32),
            pltpu.VMEM((crew, groups, 1, wide), F32),
            pltpu.SMEM((rows, groups), jnp.int32),
            pltpu.SMEM((rows, groups), jnp.int32),
            pltpu.SMEM((groups, groups), jnp.int32),
            pltpu.SMEM((crew,), jnp.int32),
            sem((3,)), sem, sem((chunks,)), sem, sem, sem, sem,
            sem, sem((rest,)), sem, sem((rest,)),
            sem, sem((chunks,)), sem, sem((chunks,)), sem, sem((paired,)), sem, sem((paired,)),
            sem, sem, sem, sem, sem, sem, sem, sem,
        ],
        compiler_params=pltpu.CompilerParams(
            collective_id=0, has_side_effects=True, vmem_limit_bytes=VMEM_GRANT
        ),
    )(stay(jnp.swapaxes(row_groups, 1, 2)), stay(col_groups), counts, stay(pieces))
    tiled = jnp.repeat(scales.reshape(plane, levels, 1, chunks, 1, LANES), wide // LANES, axis=4)
    averaged = codes.astype(F32) * tiled.reshape(plane, levels, 1, width)
    return averaged.reshape(gradients.shape), jnp.max(total.astype(jnp.int32), axis=1, keepdims=True)


def solution(mesh):
    placed = (P("row", "col", None, None, None), P("row", "col"), P(), P())
    return jax.shard_map(
        local,
        mesh=mesh,
        in_specs=placed,
        out_specs=(P("row", "col", None, None, None), P("row", "col")),
        check_vma=False,
    )
```

time: 38.1 us -> 33.7 us (0.88)
  Pallas kernels: 33.4 us -> 29.9 us
  between operations: 2.98 us -> 1.31 us
  other arithmetic: 1.41 us -> 2.18 us
    pallas_call x1, Pallas kernels: 33.4 us -> 29.9 us  [local(): pl.pallas_call(functools.partial(kernel, (across, cols, depth, levels, ch...]
    reduce_max x0 -> x1, other arithmetic: none -> 0.63 us  [local(): jnp.max(total.astype(jnp.int32), axis=1, keepdims=True)]
where the time goes in v2:
time: 33.7 us; the launch traced here: 33.5 us
  Pallas kernels  29.9 us (89%)
  other arithmetic  2.18 us (6%)
  between operations  1.31 us (4%)
    pallas_call x1, Pallas kernels, local(): pl.pallas_call(functools.partial(kernel, (across, cols, depth, levels, ch...  29.9 us
    mul x1, other arithmetic, local(): averaged = codes.astype(F32) * tiled.reshape(plane, levels, 1, width)  1.41 us

profile of v2, /device:TPU:0, one launch (start us, length us, event | category | flops | bytes accessed | tf_op | source)
XLA Modules:
  0.0 33.5 jit_solution(5031793910244707371)
XLA Ops:
  1.3 29.9 %shard_map.59 = (s16[8,2,16,1536]{3,2,1,0:T(8,128)(2,1)S(1)}, f32[8,2,1,768]{3,2,1,0:T(1,128)S(1)}, f32[1,128]{1,0:T(1,128)S(1)}) custom-call(s32[2,4,8]{2,1,0:T(4,128)} %bitcast.9, s32[1,4,8]{2,1,0:T(4,128)} %between_hbm.1, f32[1,128]{1,0:T(1,128)S(1)} %broadcast_in_dim.16.count_ref, bf16[8,2,16,1536]{3,2,1,0:T(8,128)(2,1)} %bitcast.8), custom_call_target="tpu_custom_call" | custom-call | tf_op jit(solution)/shard_map/pallas_call | solution.py:397
  31.1 0.6 %convert_reduce_fusion = s32[]{:T(128)} fusion(f32[1,128]{1,0:T(1,128)S(1)} %get-tuple-element.7), kind=kLoop, calls=%fused_computation.1 | loop fusion | flops 255 | bytes 516 | tf_op jit(solution)/shard_map/reduce_max | solution.py:455
  31.8 0.1 reduce.1
  32.0 0.1 broadcast_in_dim.18
  32.1 1.4 %convert_multiply_fusion = f32[8,2,16,1536]{3,2,1,0:T(8,128)} fusion(s16[8,2,16,1536]{3,2,1,0:T(8,128)(2,1)S(1)} %get-tuple-element.5, f32[8,2,1536]{2,1,0:T(2,128)S(1)} %broadcast_in_dim.18), kind=kLoop, calls=%fused_computation | loop fusion | flops 786432 | bytes 2457600 | tf_op jit(solution)/shard_map/mul | solution.py:454
  (3 shorter events, 0.1 us)

commit v3 on v2

--- a/solution.py
+++ b/solution.py
@@ -13,6 +13,7 @@
 JOINED = ()
 TWINNED = (0, 1)
 LEAD = 6.5
+FAR = 4.6
 JOIN_LAG = 2.2
 CROSS_LAG = 2.6
 TWIN_LAG = 2.2
@@ -74,8 +75,8 @@
 def kernel(
     geometry,
     table_hbm, between_hbm, count_ref, x_hbm,
-    out_ref, scale_ref, total_ref,
-    table, between, x_ref,
+    out_ref, spread_ref, total_ref,
+    scale_ref, table, between, x_ref,
     recv, recv_raw, own, join_out, join_out_step, join_in, join_in_step, cross_out, cross_out_step, cross_in, cross_in_step,
     codes, steps, ret, ret_scale, twin_out, twin_out_step, twin_in, twin_in_step, pick, pick_step, pair, pair_scale,
     cnt_out, cnt_in, deal_out, deal_in, weights, inverse, factor,
@@ -180,11 +181,15 @@
 
     def begin(k):
         if k not in joined:
-            for n in range(1, crew):
+            for n in range(1, plane):
                 raw_copy(k, n).start()
         else:
             for d in range(1, plane):
                 piece_copy(k, d).start()
+
+    def begin_far(k):
+        for n in range(plane, crew if k not in joined else 0):
+            raw_copy(k, n).start()
 
     def gather_raw(k):
         remote(recv_raw.at[slot[k]], recv_raw.at[slot[k]], x_send_sem, x_recv_sem.at[k], fellow_any).wait_recv()
@@ -300,6 +305,7 @@
     plan = []
     for k in range(chunks):
         plan.append((k - LEAD, 0, begin, k))
+        plan.append((k - FAR, 0, begin_far, k))
         lag = k
         if k in joined:
             plan.append((lag, 4, gather, k))
@@ -366,8 +372,13 @@
     if twinned:
         arrivals += [(pair_scale, bs_send_sem, bs_recv_sem), (pair, b_send_sem, b_recv_sem)]
     for ref, send_sem, recv_sem in arrivals:
+        remote(ref, ref, send_sem, recv_sem, fellow_any).wait_recv()
+    for q in range(plane):
+        scales = jnp.concatenate([scale_ref[q, l] for l in range(levels)], axis=0)
+        for k in range(chunks):
+            spread_ref[q, :, lanes(k)] = spread(scales[:, k * LANES:(k + 1) * LANES], wide)
+    for ref, send_sem, recv_sem in arrivals:
         remote(ref, ref, send_sem, recv_sem, fellow_any).wait_send()
-        remote(ref, ref, send_sem, recv_sem, fellow_any).wait_recv()
 
 
 def local(gradients, token_counts, row_groups, col_groups):
@@ -398,12 +409,13 @@
         functools.partial(kernel, (across, cols, depth, levels, chunks, joined, twinned, wide)),
         out_shape=(
             jax.ShapeDtypeStruct((plane, levels, height, width), jnp.int16),
-            jax.ShapeDtypeStruct((plane, levels, 1, chunks * LANES), F32),
+            jax.ShapeDtypeStruct((plane, levels, width), F32),
             jax.ShapeDtypeStruct((1, LANES), F32),
         ),
         in_specs=[hbm, hbm, vmem, hbm],
         out_specs=(vmem, vmem, vmem),
         scratch_shapes=[
+            pltpu.VMEM((plane, levels, 1, chunks * LANES), F32),
             pltpu.SMEM((2, cols, rows), jnp.int32),
             pltpu.SMEM((1, cols, rows), jnp.int32),
             pltpu.VMEM((plane, levels, height, width), gradients.dtype),
@@ -450,8 +462,7 @@
             collective_id=0, has_side_effects=True, vmem_limit_bytes=VMEM_GRANT
         ),
     )(stay(jnp.swapaxes(row_groups, 1, 2)), stay(col_groups), counts, stay(pieces))
-    tiled = jnp.repeat(scales.reshape(plane, levels, 1, chunks, 1, LANES), wide // LANES, axis=4)
-    averaged = codes.astype(F32) * tiled.reshape(plane, levels, 1, width)
+    averaged = codes.astype(F32) * scales[:, :, None, :]
     return averaged.reshape(gradients.shape), jnp.max(total.astype(jnp.int32), axis=1, keepdims=True)
 
 

time: 33.7 us -> 33.1 us (0.982)
  no operation moved by 1% of the time
where the time goes in v3:
time: 33.1 us; the launch traced here: 33 us
  Pallas kernels  29.6 us (89%)
  other arithmetic  2.04 us (6%)
  between operations  1.29 us (4%)
    pallas_call x1, Pallas kernels, local(): pl.pallas_call(functools.partial(kernel, (across, cols, depth, levels, ch...  29.6 us
    mul x1, other arithmetic, local(): averaged = codes.astype(F32) * scales[:, :, None, :]  1.41 us

profile of v3, /device:TPU:0, one launch (start us, length us, event | category | flops | bytes accessed | tf_op | source)
XLA Modules:
  0.0 33.0 jit_solution(2604524308689192758)
XLA Ops:
  1.3 29.6 %shard_map.59 = (s16[8,2,16,1536]{3,2,1,0:T(8,128)(2,1)S(1)}, f32[8,2,1536]{2,1,0:T(2,128)S(1)}, f32[1,128]{1,0:T(1,128)S(1)}) custom-call(s32[2,4,8]{2,1,0:T(4,128)} %bitcast.7, s32[1,4,8]{2,1,0:T(4,128)} %between_hbm.1, f32[1,128]{1,0:T(1,128)S(1)} %broadcast_in_dim.12.count_ref, bf16[8,2,16,1536]{3,2,1,0:T(8,128)(2,1)} %bitcast.6), custom_call_target="tpu_custom_call" | custom-call | tf_op jit(solution)/shard_map/pallas_call | solution.py:408
  30.9 0.6 %convert_reduce_fusion = s32[]{:T(128)} fusion(f32[1,128]{1,0:T(1,128)S(1)} %get-tuple-element.7), kind=kLoop, calls=%fused_computation.1 | loop fusion | flops 255 | bytes 516 | tf_op jit(solution)/shard_map/reduce_max | solution.py:466
  31.5 1.4 %convert_multiply_fusion = f32[8,2,16,1536]{3,2,1,0:T(8,128)} fusion(s16[8,2,16,1536]{3,2,1,0:T(8,128)(2,1)S(1)} %get-tuple-element.5, f32[8,2,1536]{2,1,0:T(2,128)S(1)} %get-tuple-element.6), kind=kLoop, calls=%fused_computation | loop fusion | flops 786432 | bytes 2457600 | tf_op jit(solution)/shard_map/mul | solution.py:465
  (1 shorter events, 0.0 us)

commit v4 on v3

--- a/solution.py
+++ b/solution.py
@@ -240,6 +240,8 @@
         send_cross(k, sums)
 
     def settle():
+        for n in range(crew):
+            chosen[n] = group_of(table, 1, *mate(n), cols)
         if teams > 1:
             remote(deal_in, deal_in, d_send_sem, d_recv_sem, ally(1)).wait_recv()
         for g in range(groups):
@@ -326,8 +328,6 @@
     loads[2].wait()
     path_counts(cols, table, between, second, third, paths)
     remote(cnt_in, cnt_in, n_send_sem, n_recv_sem, fellow_any).wait_recv()
-    for n in range(crew):
-        chosen[n] = group_of(table, 1, *mate(n), cols)
     parts = [None] * groups
     for n in range(crew):
         i, j = at(team * levels + (deck + levels - n // plane) % levels, (spot + plane - n % plane) % plane)

time: 33.1 us -> 33.1 us (level)
  no operation moved by 1% of the time
where the time goes in v4:
time: 33.1 us; the launch traced here: 33 us
  Pallas kernels  29.6 us (89%)
  other arithmetic  2.04 us (6%)
  between operations  1.29 us (4%)
    pallas_call x1, Pallas kernels, local(): pl.pallas_call(functools.partial(kernel, (across, cols, depth, levels, ch...  29.6 us
    mul x1, other arithmetic, local(): averaged = codes.astype(F32) * scales[:, :, None, :]  1.41 us

profile of v4, /device:TPU:0, one launch (start us, length us, event | category | flops | bytes accessed | tf_op | source)
XLA Modules:
  0.0 33.0 jit_solution(634098885196178293)
XLA Ops:
  1.3 29.6 %shard_map.59 = (s16[8,2,16,1536]{3,2,1,0:T(8,128)(2,1)S(1)}, f32[8,2,1536]{2,1,0:T(2,128)S(1)}, f32[1,128]{1,0:T(1,128)S(1)}) custom-call(s32[2,4,8]{2,1,0:T(4,128)} %bitcast.7, s32[1,4,8]{2,1,0:T(4,128)} %between_hbm.1, f32[1,128]{1,0:T(1,128)S(1)} %broadcast_in_dim.12.count_ref, bf16[8,2,16,1536]{3,2,1,0:T(8,128)(2,1)} %bitcast.6), custom_call_target="tpu_custom_call" | custom-call | tf_op jit(solution)/shard_map/pallas_call | solution.py:408
  30.9 0.6 %convert_reduce_fusion = s32[]{:T(128)} fusion(f32[1,128]{1,0:T(1,128)S(1)} %get-tuple-element.7), kind=kLoop, calls=%fused_computation.1 | loop fusion | flops 255 | bytes 516 | tf_op jit(solution)/shard_map/reduce_max | solution.py:466
  31.5 1.4 %convert_multiply_fusion = f32[8,2,16,1536]{3,2,1,0:T(8,128)} fusion(s16[8,2,16,1536]{3,2,1,0:T(8,128)(2,1)S(1)} %get-tuple-element.5, f32[8,2,1536]{2,1,0:T(2,128)S(1)} %get-tuple-element.6), kind=kLoop, calls=%fused_computation | loop fusion | flops 786432 | bytes 2457600 | tf_op jit(solution)/shard_map/mul | solution.py:465
  (1 shorter events, 0.0 us)
